TPU v7x, 128 devices: a whole 4x4x4 slice. The times are simulated.
128 devices in a mesh: row: 16 (over y, x), col: 8 (over z, core).
Axes of the slice: x: 4, y: 4, z: 4, core: 2. Of those that a mesh axis runs over, the one named last changes fastest.
Arguments:
- species: float32 [2, 512, 512, 256], P(None, None, 'row', 'col'), may hold values from -6 to 6
- coupling: float32 [2, 2], replicated, may hold values from -4 to 4
- symbol_x: float32 [512], replicated, may hold values from 0.3 to 3
- symbol_y: float32 [512], replicated, may hold values from 0.3 to 3
- symbol_z: float32 [256], replicated, may hold values from 0.3 to 3
Outputs:
- modes: float32 [2, 512, 512, 256], P(None, 'row', 'col')
All inputs are finite; a program needn't handle non-finite values.
Results may differ from a plain program's by a relative error of at most 0.000078.
Values sent between devices are 32-bit elements.
A program may use at most 128 MiB of HBM per device.

v0:
```python
import functools

import jax
import jax.numpy as jnp
import ml_dtypes
import numpy as np
from jax import lax
from jax.experimental import pallas as pl
from jax.experimental.pallas import tpu as pltpu
from jax.sharding import PartitionSpec as P

F32, BF16 = jnp.float32, jnp.bfloat16
MESH = pl.DeviceIdType.MESH
NX, NY, NZ, NF = 512, 512, 256, 2
RY, RX, CZ, CC = 4, 4, 4, 2
ROWS, COLS = RY * RX, CZ * CC
KX, KY = NX // ROWS, NY // COLS
YL, ZL = NY // ROWS, NZ // COLS
STEP = 8
PARTS = KX // STEP
CHUNKS = PARTS * NF
LAG_Y, LAG_Z = 2, 4
ROW_ORDER = (1, 4, 3, 12, 5, 15, 7, 13, 2, 8, 6, 9, 11, 14, 10)
COL_ORDER = (2, 6, 3, 7, 4, 5, 1)


def mode_table(count):
    rank = np.arange(1, count + 1)
    turns = np.outer(rank, rank) % (2 * count + 2)
    return np.sin(np.pi / (count + 1) * turns) * np.sqrt(2.0 / (count + 1))


def two_terms(table):
    high = table.astype(np.float32).astype(ml_dtypes.bfloat16)
    low = (table - high.astype(np.float64)).astype(np.float32).astype(ml_dtypes.bfloat16)
    return high, low


def tables():
    high, low = two_terms(mode_table(NX))
    pick = lambda t: t.reshape(ROWS, PARTS, STEP, NX).transpose(1, 0, 2, 3).reshape(PARTS, ROWS * STEP, NX)
    table_x = np.concatenate([pick(high), pick(low)], axis=1)
    high, low = two_terms(mode_table(NY))
    swap = lambda t: t.reshape(NY, ROWS, YL // 4, 4).transpose(0, 1, 3, 2).reshape(NY, NY)
    table_y = np.stack([swap(high), swap(low)])
    table_z = np.stack(two_terms(mode_table(NZ)))
    return table_x, table_y, table_z


def split(values):
    high = values.astype(BF16)
    return high, (values - high.astype(F32)).astype(BF16)


def dot(a, b, b_dim=0):
    return lax.dot_general(a, b, (((1,), (b_dim,)), ((), ())), preferred_element_type=F32)


def exchange_groups(values):
    lane = lax.broadcasted_iota(jnp.int32, values[0].shape, 1)
    low_half, even = lane < 64, lane % 64 < 32
    a, b, c, d = values
    a, c = jnp.where(low_half, a, pltpu.roll(c, 64, 1)), jnp.where(low_half, pltpu.roll(a, 64, 1), c)
    b, d = jnp.where(low_half, b, pltpu.roll(d, 64, 1)), jnp.where(low_half, pltpu.roll(b, 64, 1), d)
    a, b = jnp.where(even, a, pltpu.roll(b, 32, 1)), jnp.where(even, pltpu.roll(a, 96, 1), b)
    c, d = jnp.where(even, c, pltpu.roll(d, 32, 1)), jnp.where(even, pltpu.roll(c, 96, 1), d)
    return a, b, c, d


def kernel(
    coupling, sym_x, sym_y, sym_z, field, table_x, table_y, table_z, out,
    raw, high, low, tx, ty, tz, turn, row_out, row_in, col_out, col_in, base, first, result,
    load_sem, row_send, row_recv, col_send, col_recv, store_sem,
):
    row, col = lax.axis_index("row"), lax.axis_index("col")

    def row_peer(shift):
        return (row // RX + shift // RX) % RY * RX + (row + shift % RX) % RX

    def col_peer(shift):
        return (col // CC + shift // CC) % CZ * CC + (col + shift % CC) % CC

    loads = [
        pltpu.make_async_copy(field.at[0], raw.at[0], load_sem.at[0]),
        pltpu.make_async_copy(table_x, tx, load_sem.at[1]),
        pltpu.make_async_copy(field.at[1], raw.at[1], load_sem.at[2]),
        pltpu.make_async_copy(table_y, ty, load_sem.at[3]),
        pltpu.make_async_copy(table_z, tz, load_sem.at[4]),
    ]
    for load in loads:
        load.start()

    barrier = pltpu.get_barrier_semaphore()
    for shift in ROW_ORDER:
        pl.semaphore_signal(barrier, inc=1, device_id=(row_peer(shift), col), device_id_type=MESH)
    for shift in COL_ORDER:
        pl.semaphore_signal(barrier, inc=1, device_id=(row, col_peer(shift)), device_id_type=MESH)

    for block in range(NY // 128):
        lanes = jnp.broadcast_to(sym_y[:, block * 128:(block + 1) * 128], (128, 128))
        turn[0, 0:64] = jnp.transpose(lanes)[0:64]
        turn[1, 0:64] = jnp.transpose(lanes)[64:128]

        @pl.when(col // 2 == block)
        def _():
            mine = turn[col % 2]
            base[...] = 1.0 + jnp.concatenate([mine, mine], axis=1) + sym_z[...]

    def split_field(a):
        def body(n, carry):
            rows = pl.ds(pl.multiple_of(n * 128, 128), 128)
            high[a, rows, :], low[a, rows, :] = split(raw[a, rows, :])
            return carry
        lax.fori_loop(0, YL * ZL // 128, body, 0)

    def x_step(i):
        a, q = i % NF, i // NF

        def body(n, carry):
            rows = pl.ds(pl.multiple_of(n * 256, 256), 256)
            both = dot(tx[q], high[a, rows, :], 1)
            values = both[:128] + both[128:] + dot(tx[q, 0:128], low[a, rows, :], 1)
            for r in range(ROWS):
                for half in range(2):
                    turn[r, pl.ds(n * 2 + half, 8, stride=8), :] = values[r * 8:(r + 1) * 8, half * 128:(half + 1) * 128]
            return carry
        lax.fori_loop(0, YL * ZL // 256, body, 0)

        for r in range(0, ROWS, 4):
            for kb in range(2):
                parts = [turn[r:r + 4, (kb * 4 + k) * 8:(kb * 4 + k + 1) * 8, :].reshape(32, 128) for k in range(4)]
                for g, part in enumerate(exchange_groups(parts)):
                    row_out[i, r:r + 4, kb, g * 8:(g + 1) * 8, :] = part.reshape(4, 8, 128)

        for shift in ROW_ORDER:
            peer = row_peer(shift)
            pltpu.make_async_remote_copy(
                src_ref=row_out.at[i, peer], dst_ref=row_in.at[i, row], send_sem=row_send, recv_sem=row_recv.at[i],
                device_id=(peer, col), device_id_type=MESH,
            ).start()
        pltpu.make_async_copy(row_out.at[i, row], row_in.at[i, row], row_recv.at[i]).start()

    def y_step(i):
        pltpu.make_async_copy(row_in.at[i], row_in.at[i], row_recv.at[i]).wait()
        lines = jnp.concatenate([row_in[i, :, kb].reshape(NY, 128) for kb in range(2)], axis=1)
        lines_high, lines_low = split(lines)
        values = dot(ty[0], lines_high) + dot(ty[1], lines_high) + dot(ty[0], lines_low)
        for kb in range(2):
            col_out[i, :, kb] = values[:, kb * 128:(kb + 1) * 128].reshape(COLS, KY, 128)
        for shift in COL_ORDER:
            peer = col_peer(shift)
            pltpu.make_async_remote_copy(
                src_ref=col_out.at[i, peer], dst_ref=col_in.at[i, col], send_sem=col_send, recv_sem=col_recv.at[i],
                device_id=(row, peer), device_id_type=MESH,
            ).start()
        pltpu.make_async_copy(col_out.at[i, col], col_in.at[i, col], col_recv.at[i]).start()

    def z_step(i):
        a, q = i % NF, i // NF
        pltpu.make_async_copy(col_in.at[i], col_in.at[i], col_recv.at[i]).wait()

        for kb in range(2):
            halves = [exchange_groups([col_in[i, h * 4 + j, kb] for j in range(4)]) for h in range(2)]
            for k in range(4):
                lines_high, lines_low = split(jnp.concatenate([halves[0][k], halves[1][k]], axis=1))
                values = dot(lines_high, tz[0]) + dot(lines_high, tz[1]) + dot(lines_low, tz[0])
                x = kb * 4 + k

                @pl.when(a == 0)
                def _():
                    first[x] = values

                @pl.when(a == 1)
                def _():
                    other = first[x]
                    weight = 1.0 / (base[...] + sym_x[row * KX + q * STEP + x])
                    rest = 1.0 - weight
                    result[0, q * STEP + x] = weight * other + rest * (coupling[0, 0] * other + coupling[0, 1] * values)
                    result[1, q * STEP + x] = weight * values + rest * (coupling[1, 0] * other + coupling[1, 1] * values)

        @pl.when(a == 1)
        def _():
            part = pl.ds(pl.multiple_of(q * STEP, STEP), STEP)
            pltpu.make_async_copy(result.at[:, part], out.at[:, part], store_sem).start()

    loads[0].wait()
    split_field(0)
    loads[1].wait()
    pl.semaphore_wait(barrier, ROWS + COLS - 2)

    def loop(t, carry):
        @pl.when(t == 1)
        def _():
            loads[2].wait()
            split_field(1)

        @pl.when(t < CHUNKS)
        def _():
            x_step(t)

        @pl.when(t == LAG_Y)
        def _():
            loads[3].wait()

        @pl.when(jnp.logical_and(t >= LAG_Y, t < CHUNKS + LAG_Y))
        def _():
            y_step(t - LAG_Y)

        @pl.when(t == LAG_Z)
        def _():
            loads[4].wait()

        @pl.when(t >= LAG_Z)
        def _():
            z_step(t - LAG_Z)
        return carry

    lax.fori_loop(0, CHUNKS + LAG_Z, loop, 0)
    sent = row_out.at[:, pl.ds(0, ROWS - 1)]
    pltpu.make_async_copy(sent, sent, row_send).wait()
    sent = col_out.at[:, pl.ds(0, COLS - 1)]
    pltpu.make_async_copy(sent, sent, col_send).wait()
    pltpu.make_async_copy(result, out, store_sem).wait()


def local(species, coupling, symbol_x, symbol_y, symbol_z):
    field = jnp.transpose(species, (0, 2, 3, 1)).reshape(NF, YL * ZL, NX)
    smem, vmem, far = (pl.BlockSpec(memory_space=m) for m in (pltpu.SMEM, pltpu.VMEM, pl.ANY))
    return pl.pallas_call(
        kernel,
        out_shape=jax.ShapeDtypeStruct((NF, KX, KY, NZ), F32),
        in_specs=[smem, smem, vmem, vmem, far, far, far, far],
        out_specs=far,
        scratch_shapes=[
            pltpu.VMEM((NF, YL * ZL, NX), F32),
            pltpu.VMEM((NF, YL * ZL, NX), BF16),
            pltpu.VMEM((NF, YL * ZL, NX), BF16),
            pltpu.VMEM((PARTS, 2 * ROWS * STEP, NX), BF16),
            pltpu.VMEM((2, NY, NY), BF16),
            pltpu.VMEM((2, NZ, NZ), BF16),
            pltpu.VMEM((ROWS, 64, 128), F32),
            pltpu.VMEM((CHUNKS, ROWS, 2, YL, 128), F32),
            pltpu.VMEM((CHUNKS, ROWS, 2, YL, 128), F32),
            pltpu.VMEM((CHUNKS, COLS, 2, KY, 128), F32),
            pltpu.VMEM((CHUNKS, COLS, 2, KY, 128), F32),
            pltpu.VMEM((KY, NZ), F32),
            pltpu.VMEM((STEP, KY, NZ), F32),
            pltpu.VMEM((NF, KX, KY, NZ), F32),
            pltpu.SemaphoreType.DMA((5,)),
            pltpu.SemaphoreType.DMA,
            pltpu.SemaphoreType.DMA((CHUNKS,)),
            pltpu.SemaphoreType.DMA,
            pltpu.SemaphoreType.DMA((CHUNKS,)),
            pltpu.SemaphoreType.DMA,
        ],
        compiler_params=pltpu.CompilerParams(collective_id=1, has_side_effects=True, vmem_limit_bytes=52 << 20),
        name="sine_modes",
    )(coupling, symbol_x, symbol_y.reshape(1, NY), symbol_z.reshape(1, NZ), field, *map(jnp.asarray, tables()))


def solution(mesh):
    return jax.shard_map(
        local,
        mesh=mesh,
        in_specs=(P(None, None, "row", "col"), P(), P(), P(), P()),
        out_specs=P(None, "row", "col", None),
        check_vma=False,
    )
```

profile of v0, /device:TPU:1, one launch (start us, length us, event | category | flops | bytes accessed | tf_op | source)
XLA Modules:
  0.0 80.3 jit_solution(5210118846093305129)
XLA Ops:
  0.0 0.0 copy-start
  0.0 1.2 %copy-done = bf16[4,256,512]{2,1,0:T(8,128)(2,1)S(1)} copy-done((bf16[4,256,512]{2,1,0:T(8,128)(2,1)S(1)}, bf16[4,256,512]{2,1,0:T(8,128)(2,1)}, u32[]{:S(2)}) %copy-start) | copy-done | bytes 1048600
  1.2 0.0 copy-start.1
  1.2 0.9 %copy-done.1 = bf16[2,256,256]{2,1,0:T(8,128)(2,1)S(1)} copy-done((bf16[2,256,256]{2,1,0:T(8,128)(2,1)S(1)}, bf16[2,256,256]{2,1,0:T(8,128)(2,1)}, u32[]{:S(2)}) %copy-start.1) | copy-done | bytes 262168
  2.2 0.0 copy-start.2
  2.2 0.7 copy-done.2
  2.9 0.0 copy-start.3
  2.9 0.7 copy-done.3
  3.5 0.0 copy-start.4
  3.5 0.7 copy-done.4
  4.2 0.0 copy-start.5
  4.2 0.7 copy-done.5
  4.9 70.6 %sine_modes.1 = f32[2,32,64,256]{3,2,1,0:T(8,128)} custom-call(f32[2,2]{1,0:T(2,128)S(1)} %copy-done.4, f32[512]{0:T(512)S(1)} %copy-done.2, f32[1,512]{1,0:T(1,128)S(1)} %bitcast.5, f32[1,256]{1,0:T(1,128)S(1)} %bitcast.6, f32[2,1024,512]{2,1,0:T(8,128)} %bitcast.7, bf16[4,256,512]{2,1,0:T(8,128)(2,1)S(1)} %copy-done, ...), custom_call_target="tpu_custom_call" | custom-call | tf_op jit(solution)/shard_map/sine_modes/pallas_call | solution.py:229
  75.6 4.7 %copy.10 = f32[2,32,64,256]{3,2,1,0:T(8,128)} copy(f32[2,32,64,256]{3,2,1,0:T(8,128)} %sine_modes.1) | data formatting | bytes 8388608
Async XLA Ops:
  0.0 1.2 %copy-start = (bf16[4,256,512]{2,1,0:T(8,128)(2,1)S(1)}, bf16[4,256,512]{2,1,0:T(8,128)(2,1)}, u32[]{:S(2)}) copy-start(bf16[4,256,512]{2,1,0:T(8,128)(2,1)} %constant.6.clone.table_x) | copy-start | bytes 3145732
  1.2 0.9 %copy-start.1 = (bf16[2,256,256]{2,1,0:T(8,128)(2,1)S(1)}, bf16[2,256,256]{2,1,0:T(8,128)(2,1)}, u32[]{:S(2)}) copy-start(bf16[2,256,256]{2,1,0:T(8,128)(2,1)} %constant.8.clone.table_z) | copy-start | bytes 786436
  2.2 0.7 copy-start.2
  2.9 0.7 copy-start.3
  3.5 0.7 copy-start.4
  4.2 0.7 copy-start.5
where the time goes:
time: 80.5 us; the launch traced here: 80.3 us
  Pallas kernels  70.6 us (88%)
  local copies, waits for them, and re-layouts  9.59 us (12%)
    pallas_call x1, Pallas kernels, local(): pl.pallas_call(kernel, out_shape=jax.ShapeDtypeStruct((NF, KX, KY, NZ), F...  70.6 us
    unnamed x13, local copies, waits for them, and re-layouts  9.59 us

commit v1 on v0

--- a/solution.py
+++ b/solution.py
@@ -68,9 +68,9 @@
 
 
 def kernel(
-    coupling, sym_x, sym_y, sym_z, field, table_x, table_y, table_z, out,
-    raw, high, low, tx, ty, tz, turn, row_out, row_in, col_out, col_in, base, first, result,
-    load_sem, row_send, row_recv, col_send, col_recv, store_sem,
+    coupling_far, sym_x_far, sym_y_far, sym_z_far, field, table_x, table_y, table_z, result,
+    coupling, sym_x, sym_y, sym_z, raw, high, low, tx, ty, tz, turn, row_out, row_in, col_out, col_in, base, first,
+    load_sem, row_send, row_recv, col_send, col_recv,
 ):
     row, col = lax.axis_index("row"), lax.axis_index("col")
 
@@ -86,6 +86,10 @@
         pltpu.make_async_copy(field.at[1], raw.at[1], load_sem.at[2]),
         pltpu.make_async_copy(table_y, ty, load_sem.at[3]),
         pltpu.make_async_copy(table_z, tz, load_sem.at[4]),
+        pltpu.make_async_copy(sym_y_far, sym_y, load_sem.at[5]),
+        pltpu.make_async_copy(sym_z_far, sym_z, load_sem.at[6]),
+        pltpu.make_async_copy(sym_x_far, sym_x, load_sem.at[7]),
+        pltpu.make_async_copy(coupling_far, coupling, load_sem.at[8]),
     ]
     for load in loads:
         load.start()
@@ -95,16 +99,6 @@
         pl.semaphore_signal(barrier, inc=1, device_id=(row_peer(shift), col), device_id_type=MESH)
     for shift in COL_ORDER:
         pl.semaphore_signal(barrier, inc=1, device_id=(row, col_peer(shift)), device_id_type=MESH)
-
-    for block in range(NY // 128):
-        lanes = jnp.broadcast_to(sym_y[:, block * 128:(block + 1) * 128], (128, 128))
-        turn[0, 0:64] = jnp.transpose(lanes)[0:64]
-        turn[1, 0:64] = jnp.transpose(lanes)[64:128]
-
-        @pl.when(col // 2 == block)
-        def _():
-            mine = turn[col % 2]
-            base[...] = 1.0 + jnp.concatenate([mine, mine], axis=1) + sym_z[...]
 
     def split_field(a):
         def body(n, carry):
@@ -112,6 +106,17 @@
             high[a, rows, :], low[a, rows, :] = split(raw[a, rows, :])
             return carry
         lax.fori_loop(0, YL * ZL // 128, body, 0)
+
+    def make_base():
+        for load in loads[5:]:
+            load.wait()
+        for block in range(NY // 128):
+            lanes = jnp.transpose(jnp.broadcast_to(sym_y[:, block * 128:(block + 1) * 128], (128, 128)))
+
+            @pl.when(col // 2 == block)
+            def _():
+                mine = jnp.where(col % 2 == 0, lanes[0:64], lanes[64:128])
+                base[...] = 1.0 + jnp.concatenate([mine, mine], axis=1) + sym_z[...]
 
     def x_step(i):
         a, q = i % NF, i // NF
@@ -178,11 +183,6 @@
                     result[0, q * STEP + x] = weight * other + rest * (coupling[0, 0] * other + coupling[0, 1] * values)
                     result[1, q * STEP + x] = weight * values + rest * (coupling[1, 0] * other + coupling[1, 1] * values)
 
-        @pl.when(a == 1)
-        def _():
-            part = pl.ds(pl.multiple_of(q * STEP, STEP), STEP)
-            pltpu.make_async_copy(result.at[:, part], out.at[:, part], store_sem).start()
-
     loads[0].wait()
     split_field(0)
     loads[1].wait()
@@ -209,6 +209,7 @@
         @pl.when(t == LAG_Z)
         def _():
             loads[4].wait()
+            make_base()
 
         @pl.when(t >= LAG_Z)
         def _():
@@ -220,18 +221,22 @@
     pltpu.make_async_copy(sent, sent, row_send).wait()
     sent = col_out.at[:, pl.ds(0, COLS - 1)]
     pltpu.make_async_copy(sent, sent, col_send).wait()
-    pltpu.make_async_copy(result, out, store_sem).wait()
 
 
 def local(species, coupling, symbol_x, symbol_y, symbol_z):
     field = jnp.transpose(species, (0, 2, 3, 1)).reshape(NF, YL * ZL, NX)
-    smem, vmem, far = (pl.BlockSpec(memory_space=m) for m in (pltpu.SMEM, pltpu.VMEM, pl.ANY))
+    operands = (coupling, symbol_x, symbol_y.reshape(1, NY), symbol_z.reshape(1, NZ), field, *map(jnp.asarray, tables()))
+    far = pl.BlockSpec(memory_space=pltpu.HBM)
     return pl.pallas_call(
         kernel,
-        out_shape=jax.ShapeDtypeStruct((NF, KX, KY, NZ), F32),
-        in_specs=[smem, smem, vmem, vmem, far, far, far, far],
-        out_specs=far,
+        out_shape=pltpu.VMEM((NF, KX, KY, NZ), F32),
+        in_specs=[far] * 8,
+        out_specs=pl.BlockSpec(memory_space=pltpu.VMEM),
         scratch_shapes=[
+            pltpu.SMEM((NF, NF), F32),
+            pltpu.SMEM((NX,), F32),
+            pltpu.VMEM((1, NY), F32),
+            pltpu.VMEM((1, NZ), F32),
             pltpu.VMEM((NF, YL * ZL, NX), F32),
             pltpu.VMEM((NF, YL * ZL, NX), BF16),
             pltpu.VMEM((NF, YL * ZL, NX), BF16),
@@ -245,17 +250,15 @@
             pltpu.VMEM((CHUNKS, COLS, 2, KY, 128), F32),
             pltpu.VMEM((KY, NZ), F32),
             pltpu.VMEM((STEP, KY, NZ), F32),
-            pltpu.VMEM((NF, KX, KY, NZ), F32),
-            pltpu.SemaphoreType.DMA((5,)),
+            pltpu.SemaphoreType.DMA((9,)),
             pltpu.SemaphoreType.DMA,
             pltpu.SemaphoreType.DMA((CHUNKS,)),
             pltpu.SemaphoreType.DMA,
             pltpu.SemaphoreType.DMA((CHUNKS,)),
-            pltpu.SemaphoreType.DMA,
         ],
-        compiler_params=pltpu.CompilerParams(collective_id=1, has_side_effects=True, vmem_limit_bytes=52 << 20),
+        compiler_params=pltpu.CompilerParams(collective_id=1, has_side_effects=True, vmem_limit_bytes=40 << 20),
         name="sine_modes",
-    )(coupling, symbol_x, symbol_y.reshape(1, NY), symbol_z.reshape(1, NZ), field, *map(jnp.asarray, tables()))
+    )(*(pltpu.with_memory_space_constraint(operand, pltpu.HBM) for operand in operands))
 
 
 def solution(mesh):

time: 80.5 us -> 71 us (0.88)
  local copies, waits for them, and re-layouts: 9.59 us -> 2.02 us
  Pallas kernels: 70.6 us -> 68.9 us
    unnamed x13 -> x1, local copies, waits for them, and re-layouts: 9.59 us -> 2.02 us
    pallas_call x1, Pallas kernels: 70.6 us -> 68.9 us  [local(): pl.pallas_call(kernel, out_shape=pltpu.VMEM((NF, KX, KY, NZ), F32), in_sp...]
where the time goes in v1:
time: 71 us; the launch traced here: 70.9 us
  Pallas kernels  68.9 us (97%)
  local copies, waits for them, and re-layouts  2.02 us (3%)
    pallas_call x1, Pallas kernels, local(): pl.pallas_call(kernel, out_shape=pltpu.VMEM((NF, KX, KY, NZ), F32), in_sp...  68.9 us
    unnamed x1, local copies, waits for them, and re-layouts  2.02 us

profile of v1, /device:TPU:1, one launch (start us, length us, event | category | flops | bytes accessed | tf_op | source)
XLA Modules:
  0.0 70.9 jit_solution(14686123825487404105)
XLA Ops:
  0.0 68.9 %sine_modes.1 = f32[2,32,64,256]{3,2,1,0:T(8,128)S(1)} custom-call(f32[2,2]{1,0:T(2,128)} %coupling_far.1, f32[512]{0:T(512)} %sym_x_far.1, f32[1,512]{1,0:T(1,128)} %bitcast.6, f32[1,256]{1,0:T(1,128)} %bitcast.7, f32[2,1024,512]{2,1,0:T(8,128)} %bitcast.5, bf16[4,256,512]{2,1,0:T(8,128)(2,1)} %constant.6.clone.table_x, ...), custom_call_target="tpu_custom_call" | custom-call | tf_op jit(solution)/shard_map/sine_modes/pallas_call | solution.py:230
  68.9 2.0 %copy.10 = f32[2,32,64,256]{3,2,1,0:T(8,128)} copy(f32[2,32,64,256]{3,2,1,0:T(8,128)S(1)} %sine_modes.1) | data formatting | bytes 8388608

commit v2 on v1

v2 whole, which is shorter than its diff:
```python
import functools

import jax
import jax.numpy as jnp
import ml_dtypes
import numpy as np
from jax import lax
from jax.experimental import pallas as pl
from jax.experimental.pallas import tpu as pltpu
from jax.sharding import PartitionSpec as P

F32, BF16 = jnp.float32, jnp.bfloat16
MESH = pl.DeviceIdType.MESH
NX, NY, NZ, NF = 512, 512, 256, 2
RY, RX, CZ, CC = 4, 4, 4, 2
ROWS, COLS = RY * RX, CZ * CC
KX, KY = NX // ROWS, NY // COLS
YL, ZL = NY // ROWS, NZ // COLS
STEP = 8
PARTS = KX // STEP
CHUNKS = PARTS * NF
LAG_Z = 2
ROW_ORDER = (1, 4, 3, 12, 5, 15, 7, 13, 2, 8, 6, 9, 11, 14, 10)
COL_ORDER = (2, 6, 3, 7, 4, 5, 1)


def mode_table(count):
    rank = np.arange(1, count + 1)
    turns = np.outer(rank, rank) % (2 * count + 2)
    return np.sin(np.pi / (count + 1) * turns) * np.sqrt(2.0 / (count + 1))


def two_terms(table):
    high = table.astype(np.float32).astype(ml_dtypes.bfloat16)
    low = (table - high.astype(np.float64)).astype(np.float32).astype(ml_dtypes.bfloat16)
    return high, low


def tables():
    high, low = two_terms(mode_table(NX))
    pick = lambda t: t.reshape(NX, ROWS, PARTS // 2, 2, STEP).transpose(2, 0, 3, 1, 4).reshape(PARTS // 2, NX, 2 * ROWS * STEP)
    table_x = np.stack([pick(high), pick(low)], axis=1)
    high, low = two_terms(mode_table(NY))
    swap = lambda t: t.reshape(NY // 128, 128, ROWS, YL // 4, 4).transpose(0, 1, 2, 4, 3).reshape(NY // 128, 128, NY)
    table_y = np.concatenate([swap(high), swap(low)], axis=1)
    table_z = np.stack(two_terms(mode_table(NZ)))
    return table_x, table_y, table_z


def split(values):
    high = values.astype(BF16)
    return high, (values - high.astype(F32)).astype(BF16)


def dot(a, b, b_dim=0):
    return lax.dot_general(a, b, (((1,), (b_dim,)), ((), ())), preferred_element_type=F32)


def exchange_groups(values):
    lane = lax.broadcasted_iota(jnp.int32, values[0].shape, 1)
    low_half, even = lane < 64, lane % 64 < 32
    a, b, c, d = values
    a, c = jnp.where(low_half, a, pltpu.roll(c, 64, 1)), jnp.where(low_half, pltpu.roll(a, 64, 1), c)
    b, d = jnp.where(low_half, b, pltpu.roll(d, 64, 1)), jnp.where(low_half, pltpu.roll(b, 64, 1), d)
    a, b = jnp.where(even, a, pltpu.roll(b, 32, 1)), jnp.where(even, pltpu.roll(a, 96, 1), b)
    c, d = jnp.where(even, c, pltpu.roll(d, 32, 1)), jnp.where(even, pltpu.roll(c, 96, 1), d)
    return a, b, c, d


def kernel(
    coupling_far, sym_x_far, sym_y_far, sym_z_far, field, table_x, table_y, table_z, result,
    coupling, sym_x, sym_y, sym_z, raw, tx, ty, tz, turn, row_out, row_in, col_out, col_in, base,
    load_sem, row_send, row_recv, col_send, col_recv,
):
    row, col = lax.axis_index("row"), lax.axis_index("col")
    row_peers = [(row // RX + s // RX) % RY * RX + (row + s % RX) % RX for s in ROW_ORDER]
    col_peers = [(col // CC + s // CC) % CZ * CC + (col + s % CC) % CC for s in COL_ORDER]
    last = CHUNKS - 1

    pairs = [(field.at[0], raw.at[0]), (table_x.at[0], tx.at[0]), (field.at[1], raw.at[1]), (table_x.at[1], tx.at[1])]
    pairs += [(table_y, ty), (table_z, tz), (sym_y_far, sym_y), (sym_z_far, sym_z), (sym_x_far, sym_x), (coupling_far, coupling)]
    loads = [pltpu.make_async_copy(src, dst, load_sem.at[n]) for n, (src, dst) in enumerate(pairs)]
    for load in loads:
        load.start()

    barrier = pltpu.get_barrier_semaphore()
    for peer in row_peers:
        pl.semaphore_signal(barrier, inc=1, device_id=(peer, col), device_id_type=MESH)
    for peer in col_peers:
        pl.semaphore_signal(barrier, inc=1, device_id=(row, peer), device_id_type=MESH)

    def wait_bytes(ref, sem):
        pltpu.make_async_copy(ref, ref, sem).wait()

    def make_base():
        for block in range(NY // 128):
            lanes = jnp.transpose(jnp.broadcast_to(sym_y[:, block * 128:(block + 1) * 128], (128, 128)))

            @pl.when(col // 2 == block)
            def _():
                mine = jnp.where(col % 2 == 0, lanes[0:64], lanes[64:128])
                base[...] = 1.0 + jnp.concatenate([mine, mine], axis=1) + sym_z[...]

    def row_exchange(i, kbs, sem):
        for peer in row_peers:
            pltpu.make_async_remote_copy(
                src_ref=row_out.at[i, peer, *kbs], dst_ref=row_in.at[i, row, *kbs], send_sem=row_send, recv_sem=sem,
                device_id=(peer, col), device_id_type=MESH,
            ).start()
        pltpu.make_async_copy(row_out.at[i, row, *kbs], row_in.at[i, row, *kbs], sem).start()

    def col_exchange(i, kbs, sem):
        for peer in col_peers:
            pltpu.make_async_remote_copy(
                src_ref=col_out.at[i, peer, *kbs], dst_ref=col_in.at[i, col, *kbs], send_sem=col_send, recv_sem=sem,
                device_id=(row, peer), device_id_type=MESH,
            ).start()
        pltpu.make_async_copy(col_out.at[i, col, *kbs], col_in.at[i, col, *kbs], sem).start()

    def x_step(u):
        h, a = u // 2, u % 2
        for n, when in enumerate((0, 0, 1, 2)):
            pl.when(u == when)(loads[n].wait)

        def lines(n, carry):
            rows = pl.ds(pl.multiple_of(n * 128, 128), 128)
            high, low = split(raw[a, rows, :])
            both = dot(jnp.concatenate([high, low], axis=0), tx[h, 0])
            values = both[:128] + both[128:] + dot(high, tx[h, 1])
            for b in range(2):
                flipped = jnp.transpose(values[:, b * 128:(b + 1) * 128])
                for r in range(ROWS):
                    turn[b, r, pl.ds(n, 8, stride=8), :] = flipped[r * 8:(r + 1) * 8]
            return carry
        lax.fori_loop(0, YL // 4, lines, 0, unroll=2)

        for b in range(2):
            i = 2 * u + b
            for kb in range(2):
                for r in range(0, ROWS, 4):
                    parts = [turn[b, r:r + 4, (kb * 4 + k) * 8:(kb * 4 + k + 1) * 8, :].reshape(32, 128) for k in range(4)]
                    for g, part in enumerate(exchange_groups(parts)):
                        row_out[i, r:r + 4, kb, g * 8:(g + 1) * 8, :] = part.reshape(4, 8, 128)
            if b == 0:
                pl.when(u == 0)(lambda: pl.semaphore_wait(barrier, ROWS + COLS - 2))
            ends = (u == 0) if b == 0 else (u == CHUNKS // 2 - 1)

            @pl.when(ends)
            def _():
                row_exchange(i, (0,), row_recv.at[i, 0])
                row_exchange(i, (1,), row_recv.at[i, 1])

            @pl.when(jnp.logical_not(ends))
            def _():
                row_exchange(i, (), row_recv.at[i, 0])

    def y_step(i, kb, count):
        kbs = pl.ds(kb, count)
        wait_bytes(row_in.at[i, :, kbs], row_recv.at[i, kb])
        lines = jnp.concatenate([row_in[i, :, kb + k].reshape(NY, 128) for k in range(count)], axis=1)
        high, low = split(lines)
        for m in range(NY // 128):
            both = dot(ty[m], high)
            values = both[:128] + both[128:] + dot(ty[m, 0:128], low)
            for k in range(count):
                col_out[i, 2 * m:2 * m + 2, kb + k] = values[:, k * 128:(k + 1) * 128].reshape(2, KY, 128)
        col_exchange(i, (kb,) if count == 1 else (), col_recv.at[i, kb])

    def z_wait(i, kb, count):
        wait_bytes(col_in.at[i, :, pl.ds(kb, count)], col_recv.at[i, kb])

    def z_step(i, kb, count):
        a, first_x = i // 2 % 2, (i // 4 * 2 + i % 2) * STEP + kb * 4
        for k in range(count):
            halves = [exchange_groups([col_in[i, g * 4 + j, kb + k] for j in range(4)]) for g in range(2)]
            for pair in range(2):
                lines = [jnp.concatenate([halves[0][2 * pair + e], halves[1][2 * pair + e]], axis=1) for e in range(2)]
                high, low = split(jnp.concatenate(lines, axis=0))
                both = dot(jnp.concatenate([high, low], axis=0), tz[0])
                values = both[:128] + both[128:] + dot(high, tz[1])
                x = first_x + k * 4 + 2 * pair
                result[a, pl.ds(x, 2)] = values.reshape(2, KY, NZ)

        @pl.when(a == 1)
        def _():
            def mix(n, carry):
                x = first_x + n
                one, two = result[0, x], result[1, x]
                weight = 1.0 / (base[...] + sym_x[row * KX + x])
                rest = 1.0 - weight
                result[0, x] = weight * one + rest * (coupling[0, 0] * one + coupling[0, 1] * two)
                result[1, x] = weight * two + rest * (coupling[1, 0] * one + coupling[1, 1] * two)
                return carry
            lax.fori_loop(0, 4 * count, mix, 0)

    def halves(step):
        def body(kb, carry):
            step(kb)
            return carry
        lax.fori_loop(0, 2, body, 0)

    def middle(i, carry):
        pl.when(jnp.logical_or(i == 1, i == 3))(lambda: x_step((i + 3) // 2))
        y_step(i, 0, 2)

        @pl.when(i == 2)
        def _():
            z_wait(0, 0, 1)
            z_wait(0, 1, 1)

        @pl.when(i > 2)
        def _():
            z_wait(i - LAG_Z, 0, 2)

        @pl.when(i >= 2)
        def _():
            z_step(i - LAG_Z, 0, 2)
        return carry

    halves(x_step)
    for load in loads[4:]:
        load.wait()
    make_base()
    halves(lambda kb: y_step(0, kb, 1))
    lax.fori_loop(1, last, middle, 0)

    def later(i, carry):
        pl.when(i == last - 1)(lambda: halves(lambda kb: y_step(last, kb, 1)))
        z_wait(i, 0, 2)
        z_step(i, 0, 2)
        return carry
    lax.fori_loop(last - 2, last, later, 0)

    def final(kb):
        z_wait(last, kb, 1)
        z_step(last, kb, 1)
    halves(final)
    wait_bytes(row_out.at[:, pl.ds(0, ROWS - 1)], row_send)
    wait_bytes(col_out.at[:, pl.ds(0, COLS - 1)], col_send)


def local(species, coupling, symbol_x, symbol_y, symbol_z):
    field = jnp.transpose(species, (0, 2, 3, 1)).reshape(NF, YL * ZL, NX)
    operands = (coupling, symbol_x, symbol_y.reshape(1, NY), symbol_z.reshape(1, NZ), field, *map(jnp.asarray, tables()))
    far = pl.BlockSpec(memory_space=pltpu.HBM)
    return pl.pallas_call(
        kernel,
        out_shape=pltpu.VMEM((NF, KX, KY, NZ), F32),
        in_specs=[far] * 8,
        out_specs=pl.BlockSpec(memory_space=pltpu.VMEM),
        scratch_shapes=[
            pltpu.SMEM((NF, NF), F32),
            pltpu.SMEM((NX,), F32),
            pltpu.VMEM((1, NY), F32),
            pltpu.VMEM((1, NZ), F32),
            pltpu.VMEM((NF, YL * ZL, NX), F32),
            pltpu.VMEM((PARTS // 2, 2, NX, 2 * ROWS * STEP), BF16),
            pltpu.VMEM((NY // 128, 256, NY), BF16),
            pltpu.VMEM((2, NZ, NZ), BF16),
            pltpu.VMEM((2, ROWS, 64, 128), F32),
            pltpu.VMEM((CHUNKS, ROWS, 2, YL, 128), F32),
            pltpu.VMEM((CHUNKS, ROWS, 2, YL, 128), F32),
            pltpu.VMEM((CHUNKS, COLS, 2, KY, 128), F32),
            pltpu.VMEM((CHUNKS, COLS, 2, KY, 128), F32),
            pltpu.VMEM((KY, NZ), F32),
            pltpu.SemaphoreType.DMA((10,)),
            pltpu.SemaphoreType.DMA,
            pltpu.SemaphoreType.DMA((CHUNKS, 2)),
            pltpu.SemaphoreType.DMA,
            pltpu.SemaphoreType.DMA((CHUNKS, 2)),
        ],
        compiler_params=pltpu.CompilerParams(collective_id=1, has_side_effects=True, vmem_limit_bytes=40 << 20),
        name="sine_modes",
    )(*(pltpu.with_memory_space_constraint(operand, pltpu.HBM) for operand in operands))


def solution(mesh):
    return jax.shard_map(
        local,
        mesh=mesh,
        in_specs=(P(None, None, "row", "col"), P(), P(), P(), P()),
        out_specs=P(None, "row", "col", None),
        check_vma=False,
    )
```

time: 71 us -> 69.7 us (0.982)
  Pallas kernels: 68.9 us -> 67.6 us
    pallas_call x1, Pallas kernels: 68.9 us -> 67.6 us  [local(): pl.pallas_call(kernel, out_shape=pltpu.VMEM((NF, KX, KY, NZ), F32), in_sp...]
where the time goes in v2:
time: 69.7 us; the launch traced here: 69.6 us
  Pallas kernels  67.6 us (97%)
  local copies, waits for them, and re-layouts  2.02 us (3%)
    pallas_call x1, Pallas kernels, local(): pl.pallas_call(kernel, out_shape=pltpu.VMEM((NF, KX, KY, NZ), F32), in_sp...  67.6 us
    unnamed x1, local copies, waits for them, and re-layouts  2.02 us

profile of v2, /device:TPU:1, one launch (start us, length us, event | category | flops | bytes accessed | tf_op | source)
XLA Modules:
  0.0 69.6 jit_solution(9515396127157930194)
XLA Ops:
  0.0 67.6 %sine_modes.1 = f32[2,32,64,256]{3,2,1,0:T(8,128)S(1)} custom-call(f32[2,2]{1,0:T(2,128)} %coupling_far.1, f32[512]{0:T(512)} %sym_x_far.1, f32[1,512]{1,0:T(1,128)} %bitcast.6, f32[1,256]{1,0:T(1,128)} %bitcast.7, f32[2,1024,512]{2,1,0:T(8,128)} %bitcast.5, bf16[2,2,512,256]{3,2,1,0:T(8,128)(2,1)} %constant.6.clone.table_x, ...), custom_call_target="tpu_custom_call" | custom-call | tf_op jit(solution)/shard_map/sine_modes/pallas_call | solution.py:246
  67.6 2.0 %copy.10 = f32[2,32,64,256]{3,2,1,0:T(8,128)} copy(f32[2,32,64,256]{3,2,1,0:T(8,128)S(1)} %sine_modes.1) | data formatting | bytes 8388608

commit v3 on v2

--- a/solution.py
+++ b/solution.py
@@ -19,9 +19,9 @@
 STEP = 8
 PARTS = KX // STEP
 CHUNKS = PARTS * NF
-LAG_Z = 2
-ROW_ORDER = (1, 4, 3, 12, 5, 15, 7, 13, 2, 8, 6, 9, 11, 14, 10)
-COL_ORDER = (2, 6, 3, 7, 4, 5, 1)
+AHEAD, LAG_Z = 3, 3
+ROW_ORDER = (10, 6, 9, 11, 14, 5, 15, 7, 13, 2, 8, 1, 4, 3, 12)
+COL_ORDER = (4, 5, 2, 6, 3, 7, 1)
 
 
 def mode_table(count):
@@ -77,7 +77,9 @@
     col_peers = [(col // CC + s // CC) % CZ * CC + (col + s % CC) % CC for s in COL_ORDER]
     last = CHUNKS - 1
 
-    pairs = [(field.at[0], raw.at[0]), (table_x.at[0], tx.at[0]), (field.at[1], raw.at[1]), (table_x.at[1], tx.at[1])]
+    pieces = [pl.ds(n * 128, 128) for n in range(YL // 4)]
+    pairs = [(table_x.at[0], tx.at[0])] + [(field.at[0, piece], raw.at[0, piece]) for piece in pieces]
+    pairs += [(field.at[1], raw.at[1]), (table_x.at[1], tx.at[1])]
     pairs += [(table_y, ty), (table_z, tz), (sym_y_far, sym_y), (sym_z_far, sym_z), (sym_x_far, sym_x), (coupling_far, coupling)]
     loads = [pltpu.make_async_copy(src, dst, load_sem.at[n]) for n, (src, dst) in enumerate(pairs)]
     for load in loads:
@@ -119,7 +121,7 @@
 
     def x_step(u):
         h, a = u // 2, u % 2
-        for n, when in enumerate((0, 0, 1, 2)):
+        for n, when in ((0, 0), *((1 + k, 0) for k in range(8)), (9, 1), (10, 2)):
             pl.when(u == when)(loads[n].wait)
 
         def lines(n, carry):
@@ -132,7 +134,7 @@
                 for r in range(ROWS):
                     turn[b, r, pl.ds(n, 8, stride=8), :] = flipped[r * 8:(r + 1) * 8]
             return carry
-        lax.fori_loop(0, YL // 4, lines, 0, unroll=2)
+        lax.fori_loop(0, YL // 4, lines, 0, unroll=8)
 
         for b in range(2):
             i = 2 * u + b
@@ -141,18 +143,12 @@
                     parts = [turn[b, r:r + 4, (kb * 4 + k) * 8:(kb * 4 + k + 1) * 8, :].reshape(32, 128) for k in range(4)]
                     for g, part in enumerate(exchange_groups(parts)):
                         row_out[i, r:r + 4, kb, g * 8:(g + 1) * 8, :] = part.reshape(4, 8, 128)
-            if b == 0:
-                pl.when(u == 0)(lambda: pl.semaphore_wait(barrier, ROWS + COLS - 2))
-            ends = (u == 0) if b == 0 else (u == CHUNKS // 2 - 1)
-
-            @pl.when(ends)
-            def _():
-                row_exchange(i, (0,), row_recv.at[i, 0])
-                row_exchange(i, (1,), row_recv.at[i, 1])
-
-            @pl.when(jnp.logical_not(ends))
-            def _():
-                row_exchange(i, (), row_recv.at[i, 0])
+                if b * 2 + kb < AHEAD:
+                    @pl.when(u == 0)
+                    def _():
+                        if b == 0 and kb == 0:
+                            pl.semaphore_wait(barrier, ROWS + COLS - 2)
+                        row_exchange(i, (kb,), row_recv.at[i, kb])
 
     def y_step(i, kb, count):
         kbs = pl.ds(kb, count)
@@ -199,42 +195,35 @@
             return carry
         lax.fori_loop(0, 2, body, 0)
 
-    def middle(i, carry):
-        pl.when(jnp.logical_or(i == 1, i == 3))(lambda: x_step((i + 3) // 2))
-        y_step(i, 0, 2)
-
-        @pl.when(i == 2)
+    lag = LAG_Z
+
+    def send(j):
+        @pl.when(j < 2 * CHUNKS)
         def _():
-            z_wait(0, 0, 1)
-            z_wait(0, 1, 1)
-
-        @pl.when(i > 2)
+            row_exchange(j // 2, (j % 2,), row_recv.at[j // 2, j % 2])
+
+    def middle(j, carry):
+        pl.when(jnp.logical_or(j == 2, j == 6))(lambda: x_step((j + 6) // 4))
+        send(j + AHEAD)
+        y_step(j // 2, j % 2, 1)
+
+        @pl.when(j >= lag)
         def _():
-            z_wait(i - LAG_Z, 0, 2)
-
-        @pl.when(i >= 2)
-        def _():
-            z_step(i - LAG_Z, 0, 2)
+            z_wait((j - lag) // 2, (j - lag) % 2, 1)
+            z_step((j - lag) // 2, (j - lag) % 2, 1)
         return carry
 
     halves(x_step)
-    for load in loads[4:]:
+    for load in loads[11:]:
         load.wait()
     make_base()
-    halves(lambda kb: y_step(0, kb, 1))
-    lax.fori_loop(1, last, middle, 0)
-
-    def later(i, carry):
-        pl.when(i == last - 1)(lambda: halves(lambda kb: y_step(last, kb, 1)))
-        z_wait(i, 0, 2)
-        z_step(i, 0, 2)
+    lax.fori_loop(0, 2 * CHUNKS, middle, 0)
+
+    def final(j, carry):
+        z_wait(j // 2, j % 2, 1)
+        z_step(j // 2, j % 2, 1)
         return carry
-    lax.fori_loop(last - 2, last, later, 0)
-
-    def final(kb):
-        z_wait(last, kb, 1)
-        z_step(last, kb, 1)
-    halves(final)
+    lax.fori_loop(2 * CHUNKS - lag, 2 * CHUNKS, final, 0)
     wait_bytes(row_out.at[:, pl.ds(0, ROWS - 1)], row_send)
     wait_bytes(col_out.at[:, pl.ds(0, COLS - 1)], col_send)
 
@@ -263,7 +252,7 @@
             pltpu.VMEM((CHUNKS, COLS, 2, KY, 128), F32),
             pltpu.VMEM((CHUNKS, COLS, 2, KY, 128), F32),
             pltpu.VMEM((KY, NZ), F32),
-            pltpu.SemaphoreType.DMA((10,)),
+            pltpu.SemaphoreType.DMA((17,)),
             pltpu.SemaphoreType.DMA,
             pltpu.SemaphoreType.DMA((CHUNKS, 2)),
             pltpu.SemaphoreType.DMA,

time: 69.7 us -> 65.3 us (0.937)
  Pallas kernels: 67.6 us -> 63.2 us
    pallas_call x1, Pallas kernels: 67.6 us -> 63.2 us  [local(): pl.pallas_call(kernel, out_shape=pltpu.VMEM((NF, KX, KY, NZ), F32), in_sp...]
where the time goes in v3:
time: 65.3 us; the launch traced here: 65.2 us
  Pallas kernels  63.2 us (97%)
  local copies, waits for them, and re-layouts  2.02 us (3%)
    pallas_call x1, Pallas kernels, local(): pl.pallas_call(kernel, out_shape=pltpu.VMEM((NF, KX, KY, NZ), F32), in_sp...  63.2 us
    unnamed x1, local copies, waits for them, and re-layouts  2.02 us

profile of v3, /device:TPU:1, one launch (start us, length us, event | category | flops | bytes accessed | tf_op | source)
XLA Modules:
  0.0 65.2 jit_solution(5932139905262188124)
XLA Ops:
  0.0 63.2 %sine_modes.1 = f32[2,32,64,256]{3,2,1,0:T(8,128)S(1)} custom-call(f32[2,2]{1,0:T(2,128)} %coupling_far.1, f32[512]{0:T(512)} %sym_x_far.1, f32[1,512]{1,0:T(1,128)} %bitcast.6, f32[1,256]{1,0:T(1,128)} %bitcast.7, f32[2,1024,512]{2,1,0:T(8,128)} %bitcast.5, bf16[2,2,512,256]{3,2,1,0:T(8,128)(2,1)} %constant.6.clone.table_x, ...), custom_call_target="tpu_custom_call" | custom-call | tf_op jit(solution)/shard_map/sine_modes/pallas_call | solution.py:235
  63.2 2.0 %copy.10 = f32[2,32,64,256]{3,2,1,0:T(8,128)} copy(f32[2,32,64,256]{3,2,1,0:T(8,128)S(1)} %sine_modes.1) | data formatting | bytes 8388608

commit v4 on v3

--- a/solution.py
+++ b/solution.py
@@ -21,7 +21,7 @@
 CHUNKS = PARTS * NF
 AHEAD, LAG_Z = 3, 3
 ROW_ORDER = (10, 6, 9, 11, 14, 5, 15, 7, 13, 2, 8, 1, 4, 3, 12)
-COL_ORDER = (4, 5, 2, 6, 3, 7, 1)
+COL_ORDER = (5, 4, 3, 7, 2, 6, 1)
 
 
 def mode_table(count):
@@ -73,16 +73,18 @@
     load_sem, row_send, row_recv, col_send, col_recv,
 ):
     row, col = lax.axis_index("row"), lax.axis_index("col")
-    row_peers = [(row // RX + s // RX) % RY * RX + (row + s % RX) % RX for s in ROW_ORDER]
-    col_peers = [(col // CC + s // CC) % CZ * CC + (col + s % CC) % CC for s in COL_ORDER]
+    turn_of = 1 + 2 * (col % 2)
+    row_peers = [(row // RX + s // RX * turn_of) % RY * RX + (row + s % RX * turn_of) % RX for s in ROW_ORDER]
+    turn_of = 1 + 2 * (col % 2)
+    col_peers = [(col // CC + s // CC * turn_of) % CZ * CC + (col + s % CC) % CC for s in COL_ORDER]
     last = CHUNKS - 1
 
-    pieces = [pl.ds(n * 128, 128) for n in range(YL // 4)]
+    pieces = [pl.ds(n * 512, 512) for n in range(2)]
     pairs = [(table_x.at[0], tx.at[0])] + [(field.at[0, piece], raw.at[0, piece]) for piece in pieces]
     pairs += [(field.at[1], raw.at[1]), (table_x.at[1], tx.at[1])]
     pairs += [(table_y, ty), (table_z, tz), (sym_y_far, sym_y), (sym_z_far, sym_z), (sym_x_far, sym_x), (coupling_far, coupling)]
     loads = [pltpu.make_async_copy(src, dst, load_sem.at[n]) for n, (src, dst) in enumerate(pairs)]
-    for load in loads:
+    for load in loads[:3]:
         load.start()
 
     barrier = pltpu.get_barrier_semaphore()
@@ -121,8 +123,13 @@
 
     def x_step(u):
         h, a = u // 2, u % 2
-        for n, when in ((0, 0), *((1 + k, 0) for k in range(8)), (9, 1), (10, 2)):
+        for n, when in ((0, 0), (1, 0), (2, 0), (3, 1), (4, 2)):
             pl.when(u == when)(loads[n].wait)
+
+        @pl.when(u == 0)
+        def _():
+            for load in loads[3:]:
+                load.start()
 
         def lines(n, carry):
             rows = pl.ds(pl.multiple_of(n * 128, 128), 128)
@@ -155,12 +162,12 @@
         wait_bytes(row_in.at[i, :, kbs], row_recv.at[i, kb])
         lines = jnp.concatenate([row_in[i, :, kb + k].reshape(NY, 128) for k in range(count)], axis=1)
         high, low = split(lines)
+        terms = jnp.concatenate([high, low], axis=1)
         for m in range(NY // 128):
-            both = dot(ty[m], high)
-            values = both[:128] + both[128:] + dot(ty[m, 0:128], low)
-            for k in range(count):
-                col_out[i, 2 * m:2 * m + 2, kb + k] = values[:, k * 128:(k + 1) * 128].reshape(2, KY, 128)
-        col_exchange(i, (kb,) if count == 1 else (), col_recv.at[i, kb])
+            four = dot(ty[m], terms)
+            values = four[:128, :128] + (four[128:, :128] + four[:128, 128:])
+            col_out[i, 2 * m:2 * m + 2, kb] = values.reshape(2, KY, 128)
+        col_exchange(i, (kb,), col_recv.at[i, kb])
 
     def z_wait(i, kb, count):
         wait_bytes(col_in.at[i, :, pl.ds(kb, count)], col_recv.at[i, kb])
@@ -187,7 +194,7 @@
                 result[0, x] = weight * one + rest * (coupling[0, 0] * one + coupling[0, 1] * two)
                 result[1, x] = weight * two + rest * (coupling[1, 0] * one + coupling[1, 1] * two)
                 return carry
-            lax.fori_loop(0, 4 * count, mix, 0)
+            lax.fori_loop(0, 4 * count, mix, 0, unroll=4)
 
     def halves(step):
         def body(kb, carry):
@@ -214,7 +221,7 @@
         return carry
 
     halves(x_step)
-    for load in loads[11:]:
+    for load in loads[5:]:
         load.wait()
     make_base()
     lax.fori_loop(0, 2 * CHUNKS, middle, 0)
@@ -252,7 +259,7 @@
             pltpu.VMEM((CHUNKS, COLS, 2, KY, 128), F32),
             pltpu.VMEM((CHUNKS, COLS, 2, KY, 128), F32),
             pltpu.VMEM((KY, NZ), F32),
-            pltpu.SemaphoreType.DMA((17,)),
+            pltpu.SemaphoreType.DMA((11,)),
             pltpu.SemaphoreType.DMA,
             pltpu.SemaphoreType.DMA((CHUNKS, 2)),
             pltpu.SemaphoreType.DMA,

time: 65.3 us -> 64.7 us (level)
  Pallas kernels: 63.2 us -> 62.5 us
    pallas_call x1, Pallas kernels: 63.2 us -> 62.5 us  [local(): pl.pallas_call(kernel, out_shape=pltpu.VMEM((NF, KX, KY, NZ), F32), in_sp...]
where the time goes in v4:
time: 64.7 us; the launch traced here: 64.6 us
  Pallas kernels  62.5 us (97%)
  local copies, waits for them, and re-layouts  2.02 us (3%)
    pallas_call x1, Pallas kernels, local(): pl.pallas_call(kernel, out_shape=pltpu.VMEM((NF, KX, KY, NZ), F32), in_sp...  62.5 us
    unnamed x1, local copies, waits for them, and re-layouts  2.02 us

profile of v4, /device:TPU:1, one launch (start us, length us, event | category | flops | bytes accessed | tf_op | source)
XLA Modules:
  0.0 64.6 jit_solution(15798113207862770169)
XLA Ops:
  0.0 62.5 %sine_modes.1 = f32[2,32,64,256]{3,2,1,0:T(8,128)S(1)} custom-call(f32[2,2]{1,0:T(2,128)} %coupling_far.1, f32[512]{0:T(512)} %sym_x_far.1, f32[1,512]{1,0:T(1,128)} %bitcast.6, f32[1,256]{1,0:T(1,128)} %bitcast.7, f32[2,1024,512]{2,1,0:T(8,128)} %bitcast.5, bf16[2,2,512,256]{3,2,1,0:T(8,128)(2,1)} %constant.6.clone.table_x, ...), custom_call_target="tpu_custom_call" | custom-call | tf_op jit(solution)/shard_map/sine_modes/pallas_call | solution.py:242
  62.5 2.0 %copy.10 = f32[2,32,64,256]{3,2,1,0:T(8,128)} copy(f32[2,32,64,256]{3,2,1,0:T(8,128)S(1)} %sine_modes.1) | data formatting | bytes 8388608

commit v5 on v4

--- a/solution.py
+++ b/solution.py
@@ -21,7 +21,7 @@
 CHUNKS = PARTS * NF
 AHEAD, LAG_Z = 3, 3
 ROW_ORDER = (10, 6, 9, 11, 14, 5, 15, 7, 13, 2, 8, 1, 4, 3, 12)
-COL_ORDER = (5, 4, 3, 7, 2, 6, 1)
+COL_ORDER = (5, 3, 7, 4, 2, 6, 1)
 
 
 def mode_table(count):
@@ -67,9 +67,37 @@
     return a, b, c, d
 
 
+def z_transform(piece, table):
+    groups = [exchange_groups([piece(g * 4 + j) for j in range(4)]) for g in range(2)]
+    for pair in range(2):
+        lines = [jnp.concatenate([groups[0][2 * pair + e], groups[1][2 * pair + e]], axis=1) for e in range(2)]
+        high, low = split(jnp.concatenate(lines, axis=0))
+        both = dot(jnp.concatenate([high, low], axis=0), table[0])
+        yield both[:128] + both[128:] + dot(high, table[1])
+
+
+def finish(result, tail, table, weights, mixing, out, mixed, sem):
+    done = KX - 4
+    copies = [pltpu.make_async_copy(result.at[a, pl.ds(0, done)], out.at[a, pl.ds(0, done)], sem.at[a]) for a in range(NF)]
+    copies += [pltpu.make_async_copy(mixed.at[a], out.at[a, pl.ds(done, 4)], sem.at[NF + a]) for a in range(NF)]
+    for copy in copies[:NF]:
+        copy.start()
+    for pair, values in enumerate(z_transform(lambda c: tail[c], table)):
+        for e in range(2):
+            x = 2 * pair + e
+            one, two, weight = result[0, done + x], values[e * KY:(e + 1) * KY], weights[x]
+            rest = 1.0 - weight
+            mixed[0, x] = weight * one + rest * (mixing[0] * one + mixing[1] * two)
+            mixed[1, x] = weight * two + rest * (mixing[2] * one + mixing[3] * two)
+    for copy in copies[NF:]:
+        copy.start()
+    for copy in copies:
+        copy.wait()
+
+
 def kernel(
-    coupling_far, sym_x_far, sym_y_far, sym_z_far, field, table_x, table_y, table_z, result,
-    coupling, sym_x, sym_y, sym_z, raw, tx, ty, tz, turn, row_out, row_in, col_out, col_in, base,
+    coupling_far, sym_x_far, sym_y_far, sym_z_far, field, table_x, table_y, table_z, result, tail, tz, weights, mixing,
+    coupling, sym_x, sym_y, sym_z, raw, tx, ty, turn, row_out, row_in, col_out, col_in, base,
     load_sem, row_send, row_recv, col_send, col_recv,
 ):
     row, col = lax.axis_index("row"), lax.axis_index("col")
@@ -175,14 +203,8 @@
     def z_step(i, kb, count):
         a, first_x = i // 2 % 2, (i // 4 * 2 + i % 2) * STEP + kb * 4
         for k in range(count):
-            halves = [exchange_groups([col_in[i, g * 4 + j, kb + k] for j in range(4)]) for g in range(2)]
-            for pair in range(2):
-                lines = [jnp.concatenate([halves[0][2 * pair + e], halves[1][2 * pair + e]], axis=1) for e in range(2)]
-                high, low = split(jnp.concatenate(lines, axis=0))
-                both = dot(jnp.concatenate([high, low], axis=0), tz[0])
-                values = both[:128] + both[128:] + dot(high, tz[1])
-                x = first_x + k * 4 + 2 * pair
-                result[a, pl.ds(x, 2)] = values.reshape(2, KY, NZ)
+            for pair, values in enumerate(z_transform(lambda c: col_in[i, c, kb + k], tz)):
+                result[a, pl.ds(first_x + k * 4 + 2 * pair, 2)] = values.reshape(2, KY, NZ)
 
         @pl.when(a == 1)
         def _():
@@ -224,13 +246,19 @@
     for load in loads[5:]:
         load.wait()
     make_base()
+    for x in range(4):
+        weights[x] = 1.0 / (base[...] + sym_x[row * KX + KX - 4 + x])
+    for n in range(NF * NF):
+        mixing[n] = jnp.full((KY, NZ), coupling[n // NF, n % NF], F32)
     lax.fori_loop(0, 2 * CHUNKS, middle, 0)
 
     def final(j, carry):
         z_wait(j // 2, j % 2, 1)
         z_step(j // 2, j % 2, 1)
         return carry
-    lax.fori_loop(2 * CHUNKS - lag, 2 * CHUNKS, final, 0)
+    lax.fori_loop(2 * CHUNKS - lag, 2 * CHUNKS - 1, final, 0)
+    z_wait(last, 1, 1)
+    tail[...] = col_in[last, :, 1]
     wait_bytes(row_out.at[:, pl.ds(0, ROWS - 1)], row_send)
     wait_bytes(col_out.at[:, pl.ds(0, COLS - 1)], col_send)
 
@@ -239,11 +267,17 @@
     field = jnp.transpose(species, (0, 2, 3, 1)).reshape(NF, YL * ZL, NX)
     operands = (coupling, symbol_x, symbol_y.reshape(1, NY), symbol_z.reshape(1, NZ), field, *map(jnp.asarray, tables()))
     far = pl.BlockSpec(memory_space=pltpu.HBM)
-    return pl.pallas_call(
+    parts = pl.pallas_call(
         kernel,
-        out_shape=pltpu.VMEM((NF, KX, KY, NZ), F32),
+        out_shape=[
+            pltpu.VMEM((NF, KX, KY, NZ), F32),
+            pltpu.VMEM((COLS, KY, 128), F32),
+            pltpu.VMEM((2, NZ, NZ), BF16),
+            pltpu.VMEM((4, KY, NZ), F32),
+            pltpu.VMEM((NF * NF, KY, NZ), F32),
+        ],
         in_specs=[far] * 8,
-        out_specs=pl.BlockSpec(memory_space=pltpu.VMEM),
+        out_specs=[pl.BlockSpec(memory_space=pltpu.VMEM)] * 5,
         scratch_shapes=[
             pltpu.SMEM((NF, NF), F32),
             pltpu.SMEM((NX,), F32),
@@ -252,8 +286,7 @@
             pltpu.VMEM((NF, YL * ZL, NX), F32),
             pltpu.VMEM((PARTS // 2, 2, NX, 2 * ROWS * STEP), BF16),
             pltpu.VMEM((NY // 128, 256, NY), BF16),
-            pltpu.VMEM((2, NZ, NZ), BF16),
-            pltpu.VMEM((2, ROWS, 64, 128), F32),
+            pltpu.VMEM((2, ROWS, 72, 128), F32),
             pltpu.VMEM((CHUNKS, ROWS, 2, YL, 128), F32),
             pltpu.VMEM((CHUNKS, ROWS, 2, YL, 128), F32),
             pltpu.VMEM((CHUNKS, COLS, 2, KY, 128), F32),
@@ -268,6 +301,15 @@
         compiler_params=pltpu.CompilerParams(collective_id=1, has_side_effects=True, vmem_limit_bytes=40 << 20),
         name="sine_modes",
     )(*(pltpu.with_memory_space_constraint(operand, pltpu.HBM) for operand in operands))
+    return pl.pallas_call(
+        finish,
+        out_shape=pltpu.HBM((NF, KX, KY, NZ), F32),
+        in_specs=[pl.BlockSpec(memory_space=pltpu.VMEM)] * 5,
+        out_specs=far,
+        scratch_shapes=[pltpu.VMEM((NF, 4, KY, NZ), F32), pltpu.SemaphoreType.DMA((2 * NF,))],
+        compiler_params=pltpu.CompilerParams(vmem_limit_bytes=8 << 20),
+        name="finish",
+    )(*(pltpu.with_memory_space_constraint(part, pltpu.VMEM) for part in parts))
 
 
 def solution(mesh):

time: 64.7 us -> 64.1 us (level)
  local copies, waits for them, and re-layouts: 2.02 us -> 0 us
  Pallas kernels: 62.5 us -> 64 us
    unnamed x1 -> x0, local copies, waits for them, and re-layouts: 2.02 us -> none
    pallas_call x1 -> x2, Pallas kernels: 62.5 us -> 64 us  [the longest x1 61.9 us: local(): pl.pallas_call(kernel, out_shape=[pltpu.VMEM((NF, KX, KY, NZ), F32), pltp...]
where the time goes in v5:
time: 64.1 us; the launch traced here: 64 us
  Pallas kernels  64 us (100%)
    pallas_call x1, Pallas kernels, local(): pl.pallas_call(kernel, out_shape=[pltpu.VMEM((NF, KX, KY, NZ), F32), pltp...  61.9 us
    pallas_call x1, Pallas kernels, local(): pl.pallas_call(finish, out_shape=pltpu.HBM((NF, KX, KY, NZ), F32), in_spe...  2.03 us

profile of v5, /device:TPU:1, one launch (start us, length us, event | category | flops | bytes accessed | tf_op | source)
XLA Modules:
  0.0 64.0 jit_solution(4357973325742137900)
XLA Ops:
  0.0 61.9 %sine_modes.1 = (f32[2,32,64,256]{3,2,1,0:T(8,128)S(1)}, f32[8,64,128]{2,1,0:T(8,128)S(1)}, bf16[2,256,256]{2,1,0:T(8,128)(2,1)S(1)}, f32[4,64,256]{2,1,0:T(8,128)S(1)}, f32[4,64,256]{2,1,0:T(8,128)S(1)}) custom-call(f32[2,2]{1,0:T(2,128)} %coupling_far.1, f32[512]{0:T(512)} %sym_x_far.1, f32[1,512]{1,0:T(1,128)} %bitcast.6, f32[1,256]{1,0:T(1,128)} %bitcast.7, ...), custom_call_target="tpu_custom_call" | custom-call | tf_op jit(solution)/shard_map/sine_modes/pallas_call | solution.py:270
  61.9 2.0 %finish.1 = f32[2,32,64,256]{3,2,1,0:T(8,128)} custom-call(f32[2,32,64,256]{3,2,1,0:T(8,128)S(1)} %get-tuple-element.10.result, f32[8,64,128]{2,1,0:T(8,128)S(1)} %get-tuple-element.11.tail, bf16[2,256,256]{2,1,0:T(8,128)(2,1)S(1)} %get-tuple-element.12.table, f32[4,64,256]{2,1,0:T(8,128)S(1)} %get-tuple-element.13.weights, ...), custom_call_target="tpu_custom_call" | custom-call | tf_op jit(solution)/shard_map/finish/pallas_call | solution.py:304

commit v6 on v5

--- a/solution.py
+++ b/solution.py
@@ -20,7 +20,7 @@
 PARTS = KX // STEP
 CHUNKS = PARTS * NF
 AHEAD, LAG_Z = 3, 3
-ROW_ORDER = (10, 6, 9, 11, 14, 5, 15, 7, 13, 2, 8, 1, 4, 3, 12)
+ROW_ORDER = (10, 6, 9, 14, 11, 2, 8, 5, 15, 7, 13, 1, 4, 3, 12)
 COL_ORDER = (5, 3, 7, 4, 2, 6, 1)
 
 

time: 64.1 us -> 64.2 us (level)
  no operation moved by 1% of the time
where the time goes in v6:
time: 64.2 us; the launch traced here: 64.1 us
  Pallas kernels  64 us (100%)
    pallas_call x1, Pallas kernels, local(): pl.pallas_call(kernel, out_shape=[pltpu.VMEM((NF, KX, KY, NZ), F32), pltp...  62 us
    pallas_call x1, Pallas kernels, local(): pl.pallas_call(finish, out_shape=pltpu.HBM((NF, KX, KY, NZ), F32), in_spe...  2.03 us

profile of v6, /device:TPU:1, one launch (start us, length us, event | category | flops | bytes accessed | tf_op | source)
XLA Modules:
  0.0 64.1 jit_solution(6178956479496727754)
XLA Ops:
  0.0 62.0 %sine_modes.1 = (f32[2,32,64,256]{3,2,1,0:T(8,128)S(1)}, f32[8,64,128]{2,1,0:T(8,128)S(1)}, bf16[2,256,256]{2,1,0:T(8,128)(2,1)S(1)}, f32[4,64,256]{2,1,0:T(8,128)S(1)}, f32[4,64,256]{2,1,0:T(8,128)S(1)}) custom-call(f32[2,2]{1,0:T(2,128)} %coupling_far.1, f32[512]{0:T(512)} %sym_x_far.1, f32[1,512]{1,0:T(1,128)} %bitcast.6, f32[1,256]{1,0:T(1,128)} %bitcast.7, ...), custom_call_target="tpu_custom_call" | custom-call | tf_op jit(solution)/shard_map/sine_modes/pallas_call | solution.py:270
  62.0 2.0 %finish.1 = f32[2,32,64,256]{3,2,1,0:T(8,128)} custom-call(f32[2,32,64,256]{3,2,1,0:T(8,128)S(1)} %get-tuple-element.10.result, f32[8,64,128]{2,1,0:T(8,128)S(1)} %get-tuple-element.11.tail, bf16[2,256,256]{2,1,0:T(8,128)(2,1)S(1)} %get-tuple-element.12.table, f32[4,64,256]{2,1,0:T(8,128)S(1)} %get-tuple-element.13.weights, ...), custom_call_target="tpu_custom_call" | custom-call | tf_op jit(solution)/shard_map/finish/pallas_call | solution.py:304
